TPU v7x, 32 devices: a whole 2x2x4 slice. The times are simulated.
32 devices in a mesh: ep: 4 (over y, x), fsdp: 8 (over z, core).
Axes of the slice: x: 2, y: 2, z: 4, core: 2. Of those that a mesh axis runs over, the one named last changes fastest.
Arguments:
- train_gate: float32 [64, 2048, 1408], P('ep', 'fsdp'), may hold values from -0.1875 to 0.1875
- other_gate: bfloat16 [64, 2048, 1408], P('ep', 'fsdp'), may hold values from -0.0625 to 0.0625
- train_up: float32 [64, 2048, 1408], P('ep', 'fsdp'), may hold values from -0.1875 to 0.1875
- other_up: bfloat16 [64, 2048, 1408], P('ep', 'fsdp'), may hold values from -0.0625 to 0.0625
- router_weight: float32 [2048, 64], P('fsdp', 'ep'), may hold values from -0.125 to 0.125
- router_gain: float32 [2048], P('fsdp'), may hold values from 0.25 to 1.75
Outputs:
- ready_gate: bfloat16 [64, 2048, 1408], P('ep', None, 'fsdp')
- ready_up: bfloat16 [64, 2048, 1408], P('ep', None, 'fsdp')
- scale_gate: float32 [64, 1408], P('ep', 'fsdp')
- scale_up: float32 [64, 1408], P('ep', 'fsdp')
- serve_router: bfloat16 [2048, 64], replicated
All inputs are finite; a program needn't handle non-finite values. Where the computation divides by a largest or mean magnitude, that divisor is 1e-20 or more.
Results may differ from a plain program's by a relative error of at most 0.001.
Values may be sent and summed in bfloat16 or wider, within the bound.
No kernel may reach another device: no remote copies, remote signals or barrier semaphores. Data moves between devices by JAX's collectives and lax.ppermute only.
A program may use at most 192 MiB of HBM per device.

v0:
```python
import jax
import jax.numpy as jnp
from jax import lax
from jax.sharding import PartitionSpec as P


def per_device(train_gate, other_gate, train_up, other_up, router_weight, router_gain):
    latest_gate = train_gate + other_gate.astype(jnp.float32)
    latest_up = train_up + other_up.astype(jnp.float32)
    scale_gate, scale_up = lax.pmax(
        (jnp.max(jnp.abs(latest_gate), axis=1), jnp.max(jnp.abs(latest_up), axis=1)), "fsdp"
    )
    narrow_gate, narrow_up = (
        (latest_gate / jnp.expand_dims(scale_gate, 1)).astype(jnp.bfloat16),
        (latest_up / jnp.expand_dims(scale_up, 1)).astype(jnp.bfloat16),
    )
    ready_gate, ready_up = (
        lax.all_to_all(narrow_gate, "fsdp", split_axis=2, concat_axis=1, tiled=True),
        lax.all_to_all(narrow_up, "fsdp", split_axis=2, concat_axis=1, tiled=True),
    )
    scale_gate = lax.dynamic_slice_in_dim(
        scale_gate, lax.axis_index("fsdp") * ready_gate.shape[2], ready_gate.shape[2], axis=1
    )
    scale_up = lax.dynamic_slice_in_dim(
        scale_up, lax.axis_index("fsdp") * ready_up.shape[2], ready_up.shape[2], axis=1
    )
    part_router = (router_weight * router_gain[:, None]).astype(jnp.bfloat16)
    row_router = lax.all_gather(part_router, "fsdp", axis=0, tiled=True)
    serve_router = lax.all_gather(row_router, "ep", axis=1, tiled=True)
    return (ready_gate, ready_up, scale_gate, scale_up, serve_router)


def solution(mesh):
    in_specs = (
        P("ep", "fsdp", None),
        P("ep", "fsdp", None),
        P("ep", "fsdp", None),
        P("ep", "fsdp", None),
        P("fsdp", "ep"),
        P("fsdp"),
    )
    out_specs = (
        P("ep", None, "fsdp"),
        P("ep", None, "fsdp"),
        P("ep", "fsdp"),
        P("ep", "fsdp"),
        P(),
    )
    return jax.shard_map(
        per_device, mesh=mesh, in_specs=in_specs, out_specs=out_specs, check_vma=False
    )
```

profile of v0, /device:TPU:0, one launch (start us, length us, event | category | flops | bytes accessed | tf_op | source)
XLA Modules:
  0.0 809.5 jit_solution(1631548331659294860)
XLA Ops:
  7.2 0.0 all-reduce.3.cloned.1.call-start
  7.2 23.7 %copy.38 = f32[16,256,1408]{1,0,2:T(8,128)} copy(f32[16,256,1408]{2,1,0:T(8,128)} %param.8) | data formatting | bytes 46137344 | tf_op args[2]
  30.9 16.4 %copy.37 = bf16[16,256,1408]{1,0,2:T(8,128)(2,1)} copy(bf16[16,256,1408]{2,1,0:T(8,128)(2,1)} %param.9) | data formatting | bytes 23068672 | tf_op args[3]
  47.2 23.7 %copy.34 = f32[16,256,1408]{1,0,2:T(8,128)} copy(f32[16,256,1408]{2,1,0:T(8,128)} %param.6) | data formatting | bytes 46137344 | tf_op args[0]
  70.9 16.4 %copy.33 = bf16[16,256,1408]{1,0,2:T(8,128)(2,1)} copy(bf16[16,256,1408]{2,1,0:T(8,128)(2,1)} %param.7) | data formatting | bytes 23068672 | tf_op args[1]
  87.3 0.0 copy-start
  87.3 0.0 copy-start.1
  87.3 20.8 %abs_reduce_fusion = f32[16,1408]{0,1:T(8,128)} fusion(f32[16,256,1408]{1,0,2:T(8,128)} %copy.38, bf16[16,256,1408]{1,0,2:T(8,128)(2,1)} %copy.37), kind=kLoop, calls=%fused_computation.1 | loop fusion | flops 23046144 | bytes 34693120 | tf_op jit(solution)/shard_map/reduce_max | solution.py:11
  108.1 0.0 copy-done
  108.1 0.0 copy-done.1
  108.1 14.9 %abs_reduce_fusion.1 = f32[16,1408]{0,1:T(8,128)} fusion(f32[16,256,1408]{1,0,2:T(8,128)S(1)} %copy-done, bf16[16,256,1408]{1,0,2:T(8,128)(2,1)S(1)} %copy-done.1), kind=kLoop, calls=%fused_computation.4 | loop fusion | flops 23046144 | bytes 34693120 | tf_op jit(solution)/shard_map/reduce_max | solution.py:11
  123.0 0.0 all-reduce.3.cloned.1.call-update
  123.0 64.1 %all-reduce.3.cloned.1.call-done = (f32[16,1408]{0,1:T(8,128)}, f32[16,1408]{0,1:T(8,128)}) async-done(((f32[16,1408]{0,1:T(8,128)}, f32[16,1408]{0,1:T(8,128)}), (f32[16,1408]{0,1:T(8,128)}, f32[16,1408]{0,1:T(8,128)})) %all-reduce.3.cloned.1.call-update) | async-done | bytes 180240 | tf_op jit(solution)/shard_map/pmax | solution.py:10
  187.2 27.3 %divide_convert_fusion = (bf16[16,256,1408]{1,0,2:T(8,128)(2,1)}, bf16[16,256,1408]{1,0,2:T(8,128)(2,1)S(1)}) fusion(f32[16,256,1408]{1,0,2:T(8,128)} %copy.38, bf16[16,256,1408]{1,0,2:T(8,128)(2,1)} %copy.37, f32[16,1408]{0,1:T(8,128)} %get-tuple-element.11, f32[16,1408]{0,1:T(8,128)} %get-tuple-element.10, f32[16,256,1408]{1,0,2:T(8,128)} %copy.34, ...), kind=kLoop, calls=%fused_computation | loop fusion | flops 46137344 | bytes 92454912 | tf_op jit(solution)/shard_map/convert_element_type | solution.py:15
  214.5 0.0 copy-start.2
  214.5 0.0 copy-start.3
  214.5 255.0 %all_to_all.36 = bf16[16,256,1408]{1,0,2:T(8,128)(2,1)} all-to-all(bf16[16,256,1408]{1,0,2:T(8,128)(2,1)S(1)} %get-tuple-element.13), channel_id=1, replica_groups=mesh['ep'=4,'fsdp'=8] {'fsdp'}, dimensions={2} | all-to-all | bytes 23068672 | tf_op jit(solution)/shard_map/all_to_all | solution.py:18
  469.5 5.3 all-to-all-start.1
  474.8 0.0 copy-done.2
  474.8 0.0 copy-done.3
  474.8 257.3 %all_gather.6 = bf16[2048,16]{0,1:T(8,128)(2,1)S(1)} all-gather(bf16[256,16]{0,1:T(8,128)(2,1)S(1)} %multiply_convert_fusion), channel_id=1, replica_groups=mesh['ep'=4,'fsdp'=8] {'fsdp'}, dimensions={0}, use_global_device_ids=true | all-gather | bytes 73728 | tf_op jit(solution)/shard_map/all_gather | solution.py:28
  732.1 8.9 %all_gather.7 = bf16[2048,64]{0,1:T(8,128)(2,1)S(1)} all-gather(bf16[2048,16]{0,1:T(8,128)(2,1)S(1)} %all_gather.6), channel_id=1, replica_groups=mesh['ep'=4,'fsdp'=8] {'ep'}, dimensions={1}, use_global_device_ids=true | all-gather | bytes 327680 | tf_op jit(solution)/shard_map/all_gather | solution.py:29
  741.0 0.9 constant_dynamic-slice_fusion
  742.0 0.7 copy.41
  742.6 0.7 copy.42
  743.3 11.3 %copy.36 = bf16[16,8,256,176]{2,1,3,0:T(8,128)(2,1)} copy(bf16[16,8,256,176]{2,0,3,1:T(8,128)(2,1)} %bitcast.14) | data formatting | bytes 23068672 | tf_op jit(solution)/shard_map/all_to_all | solution.py:18
  754.7 18.0 %all_to_all.29 = bf16[16,2048,176]{1,2,0:T(8,128)(2,1)} reshape(bf16[16,8,256,176]{2,1,3,0:T(8,128)(2,1)} %copy.36) | data formatting | bytes 23068672 | tf_op jit(solution)/shard_map/all_to_all | solution.py:18
  772.6 0.0 all-to-all-done.1
  772.6 11.4 %copy.40 = bf16[16,8,256,176]{2,1,3,0:T(8,128)(2,1)} copy(bf16[16,8,256,176]{2,0,3,1:T(8,128)(2,1)} %bitcast.5) | data formatting | bytes 23068672 | tf_op jit(solution)/shard_map/all_to_all | solution.py:19
  784.0 18.0 %all_to_all.33 = bf16[16,2048,176]{1,2,0:T(8,128)(2,1)} reshape(bf16[16,8,256,176]{2,1,3,0:T(8,128)(2,1)} %copy.40) | data formatting | bytes 23068672 | tf_op jit(solution)/shard_map/all_to_all | solution.py:19
  802.0 0.7 copy.48
  (1 shorter events, 0.0 us)
Async XLA Ops:
  7.2 180.0 %all-reduce.3.cloned.1.call-start = ((), (), s32[]{:S(2)}) async-start(), calls=%async_computation.2 | async-start | bytes 2883584 | tf_op jit(solution)/shard_map/pmax | solution.py:10
  87.3 20.8 %copy-start = (f32[16,256,1408]{1,0,2:T(8,128)S(1)}, f32[16,256,1408]{1,0,2:T(8,128)}, u32[]{:S(2)}) copy-start(f32[16,256,1408]{1,0,2:T(8,128)} %copy.34) | copy-start | bytes 69206016
  87.3 20.9 %copy-start.1 = (bf16[16,256,1408]{1,0,2:T(8,128)(2,1)S(1)}, bf16[16,256,1408]{1,0,2:T(8,128)(2,1)}, u32[]{:S(2)}) copy-start(bf16[16,256,1408]{1,0,2:T(8,128)(2,1)} %copy.33) | copy-start | bytes 34603012
  214.5 260.3 %copy-start.2 = (f32[256,16]{0,1:T(8,128)S(1)}, f32[256,16]{0,1:T(8,128)}, u32[]{:S(2)}) copy-start(f32[256,16]{0,1:T(8,128)} %param.10) | copy-start | bytes 49156
  214.5 260.3 %copy-start.3 = (f32[256]{0:T(256)S(1)}, f32[256]{0:T(256)}, u32[]{:S(2)}) copy-start(f32[256]{0:T(256)} %param.11) | copy-start | bytes 3076
  469.5 303.1 %all-to-all-start.1 = ((bf16[16,256,1408]{1,0,2:T(8,128)(2,1)}), bf16[16,256,1408]{1,0,2:T(8,128)(2,1)}, u32[]{:S(2)}, u32[]{:S(2)}) async-start(bf16[16,256,1408]{1,0,2:T(8,128)(2,1)} %get-tuple-element.12), calls=%async_computation.1 | async-start | bytes 23068672 | tf_op jit(solution)/shard_map/all_to_all | solution.py:19
Sparse Core Ops, SparseCore 0:
  123.2 63.9 all-reduce.2
where the time goes:
time: 812 us; the launch traced here: 810 us
  blocking collectives  521 us (64%)
  local copies, waits for them, and re-layouts  142 us (17%)
  waiting for transfers between devices  64.2 us (8%)
  other arithmetic  63 us (8%)
  between operations  14.1 us (2%)
    all_gather x1, blocking collectives, per_device(): row_router = lax.all_gather(part_router, 'fsdp', axis=0, tiled=True)  257 us
    all_to_all x1, blocking collectives, per_device(): lax.all_to_all(narrow_gate, 'fsdp', split_axis=2, concat_axis=1, tiled=True)  255 us
    unnamed x15, local copies, waits for them, and re-layouts  82.2 us
    pmax x1, waiting for transfers between devices, per_device(): lax.pmax((jnp.max(jnp.abs(latest_gate), axis=1), jnp.max(jnp.abs(latest_u...  64.1 us
    all_to_all x2, local copies, waits for them, and re-layouts, per_device(): lax.all_to_all(narrow_up, 'fsdp', split_axis=2, concat_axis=1, tiled=True)  29.3 us
    all_to_all x2, local copies, waits for them, and re-layouts, per_device(): lax.all_to_all(narrow_gate, 'fsdp', split_axis=2, concat_axis=1, tiled=True)  29.3 us
    convert_element_type x1, other arithmetic, per_device(): (latest_up / jnp.expand_dims(scale_up, 1)).astype(jnp.bfloat16)  27.3 us
    reduce_max x1, other arithmetic, per_device(): jnp.max(jnp.abs(latest_up), axis=1)  20.8 us
  transfers between devices with their start and end apart: 2, of which 1 were waited for; matrix products, arithmetic and copies ran while one was open for 2% of the time, Pallas kernels for 0%

commit v1 on v0

--- a/solution.py
+++ b/solution.py
@@ -2,6 +2,7 @@
 import jax.numpy as jnp
 from jax import lax
 from jax.sharding import PartitionSpec as P
+from jax.lax import all_to_all, axis_size
 
 
 def per_device(train_gate, other_gate, train_up, other_up, router_weight, router_gain):
@@ -15,7 +16,12 @@
         (latest_up / jnp.expand_dims(scale_up, 1)).astype(jnp.bfloat16),
     )
     ready_gate, ready_up = (
-        lax.all_to_all(narrow_gate, "fsdp", split_axis=2, concat_axis=1, tiled=True),
+        jnp.concatenate(
+            all_to_all(
+                jnp.stack(jnp.split(narrow_gate, axis_size("fsdp"), axis=2), axis=0), "fsdp", 0, 0
+            ),
+            axis=1,
+        ),
         lax.all_to_all(narrow_up, "fsdp", split_axis=2, concat_axis=1, tiled=True),
     )
     scale_gate = lax.dynamic_slice_in_dim(

time: 812 us -> 776 us (0.956)
  blocking collectives: 521 us -> 266 us
  waiting for transfers between devices: 64.2 us -> 295 us
  local copies, waits for them, and re-layouts: 142 us -> 130 us
    all_to_all x1 -> x0, blocking collectives: 255 us -> none  [per_device(): lax.all_to_all(narrow_gate, 'fsdp', split_axis=2, concat_axis=1, tiled=True)]
    all_to_all x0 -> x1, waiting for transfers between devices: none -> 235 us  [per_device(): all_to_all(jnp.stack(jnp.split(narrow_gate, axis_size('fsdp'), axis=2), a...]
    all_to_all x2 -> x0, local copies, waits for them, and re-layouts: 29.3 us -> none  [per_device(): lax.all_to_all(narrow_gate, 'fsdp', split_axis=2, concat_axis=1, tiled=True)]
    convert_element_type x0 -> x1, other arithmetic: none -> 12 us  [per_device(): (latest_gate / jnp.expand_dims(scale_gate, 1)).astype(jnp.bfloat16)]
    convert_element_type x1, other arithmetic: 27.3 us -> 16.6 us  [per_device(): (latest_up / jnp.expand_dims(scale_up, 1)).astype(jnp.bfloat16)]
    reshape x0 -> x1, local copies, waits for them, and re-layouts: none -> 10 us  [per_device(): jnp.concatenate(all_to_all(jnp.stack(jnp.split(narrow_gate, axis_size('fs...]
    unnamed x15 -> x23, local copies, waits for them, and re-layouts: 82.2 us -> 88.1 us
  transfers between devices with their start and end apart: 2 -> 3, of which waited for: 1 -> 2; matrix products, arithmetic and copies ran while one was open for 2% -> 4% of each run, Pallas kernels for 0% -> 0%
where the time goes in v1:
time: 776 us; the launch traced here: 773 us
  waiting for transfers between devices  295 us (38%)
  blocking collectives  266 us (34%)
  local copies, waits for them, and re-layouts  130 us (17%)
  other arithmetic  57.4 us (7%)
  between operations  14.1 us (2%)
  starting transfers between devices  10.7 us (1%)
    all_gather x1, blocking collectives, per_device(): row_router = lax.all_gather(part_router, 'fsdp', axis=0, tiled=True)  257 us
    all_to_all x1, waiting for transfers between devices, per_device(): all_to_all(jnp.stack(jnp.split(narrow_gate, axis_size('fsdp'), axis=2), a...  235 us
    unnamed x23, local copies, waits for them, and re-layouts  88.1 us
    pmax x1, waiting for transfers between devices, per_device(): lax.pmax((jnp.max(jnp.abs(latest_gate), axis=1), jnp.max(jnp.abs(latest_u...  60.2 us
    all_to_all x2, local copies, waits for them, and re-layouts, per_device(): lax.all_to_all(narrow_up, 'fsdp', split_axis=2, concat_axis=1, tiled=True)  29.3 us
    reduce_max x1, other arithmetic, per_device(): jnp.max(jnp.abs(latest_up), axis=1)  20.8 us
    convert_element_type x1, other arithmetic, per_device(): (latest_up / jnp.expand_dims(scale_up, 1)).astype(jnp.bfloat16)  16.6 us
  transfers between devices with their start and end apart: 3, of which 2 were waited for; matrix products, arithmetic and copies ran while one was open for 4% of the time, Pallas kernels for 0%

profile of v1, /device:TPU:0, one launch (start us, length us, event | category | flops | bytes accessed | tf_op | source)
XLA Modules:
  0.0 773.4 jit_solution(17048523216744664075)
XLA Ops:
  7.2 0.0 all-reduce.3.cloned.1.call-start
  7.2 23.7 %copy.39 = f32[16,256,1408]{1,0,2:T(8,128)} copy(f32[16,256,1408]{2,1,0:T(8,128)} %param.8) | data formatting | bytes 46137344 | tf_op args[2]
  30.9 16.4 %copy.38 = bf16[16,256,1408]{1,0,2:T(8,128)(2,1)} copy(bf16[16,256,1408]{2,1,0:T(8,128)(2,1)} %param.9) | data formatting | bytes 23068672 | tf_op args[3]
  47.2 23.3 %copy.36 = f32[16,256,1408]{1,2,0:T(8,128)} copy(f32[16,256,1408]{2,1,0:T(8,128)} %param.6) | data formatting | bytes 46137344 | tf_op args[0]
  70.5 15.0 %copy.35 = bf16[16,256,1408]{1,2,0:T(8,128)(2,1)} copy(bf16[16,256,1408]{2,1,0:T(8,128)(2,1)} %param.7) | data formatting | bytes 23068672 | tf_op args[1]
  85.5 0.0 copy-start
  85.5 0.0 copy-start.1
  85.5 20.8 %abs_reduce_fusion = f32[16,1408]{0,1:T(8,128)} fusion(f32[16,256,1408]{1,0,2:T(8,128)} %copy.39, bf16[16,256,1408]{1,0,2:T(8,128)(2,1)} %copy.38), kind=kLoop, calls=%fused_computation.1 | loop fusion | flops 23046144 | bytes 34693120 | tf_op jit(solution)/shard_map/reduce_max | solution.py:12
  106.4 0.0 copy-done
  106.4 0.0 copy-done.1
  106.4 7.9 %abs_reduce_fusion.1 = f32[16,1408]{1,0:T(8,128)} fusion(f32[16,256,1408]{1,2,0:T(8,128)S(1)} %copy-done, bf16[16,256,1408]{1,2,0:T(8,128)(2,1)S(1)} %copy-done.1), kind=kLoop, calls=%fused_computation.4 | loop fusion | flops 23046144 | bytes 34693120 | tf_op jit(solution)/shard_map/reduce_max | solution.py:12
  114.3 0.0 all-reduce.3.cloned.1.call-update
  114.3 60.2 %all-reduce.3.cloned.1.call-done = (f32[16,1408]{1,0:T(8,128)}, f32[16,1408]{0,1:T(8,128)}) async-done(((f32[16,1408]{1,0:T(8,128)}, f32[16,1408]{0,1:T(8,128)}), (f32[16,1408]{1,0:T(8,128)}, f32[16,1408]{0,1:T(8,128)})) %all-reduce.3.cloned.1.call-update) | async-done | bytes 180240 | tf_op jit(solution)/shard_map/pmax | solution.py:11
  174.5 12.0 %divide_convert_fusion.1 = bf16[16,256,1408]{1,2,0:T(8,128)(2,1)S(1)} fusion(f32[16,256,1408]{1,2,0:T(8,128)} %copy.36, bf16[16,256,1408]{1,2,0:T(8,128)(2,1)} %copy.35, f32[16,1408]{1,0:T(8,128)} %get-tuple-element.10), kind=kLoop, calls=%fused_computation.3 | loop fusion | flops 23068672 | bytes 46227456 | tf_op jit(solution)/shard_map/convert_element_type | solution.py:15
  186.6 1.2 fusion.7
  187.8 1.2 fusion.6
  189.0 1.2 fusion.5
  190.2 1.2 fusion.4
  191.4 1.2 fusion.3
  192.6 1.2 fusion.2
  193.8 1.2 fusion.1
  195.0 1.2 fusion
  196.2 0.0 copy-start.2
  196.2 5.4 all-to-all-start
  201.6 0.0 copy-done.2
  201.6 16.6 %divide_convert_fusion = bf16[16,256,1408]{1,0,2:T(8,128)(2,1)} fusion(f32[16,256,1408]{1,0,2:T(8,128)} %copy.39, bf16[16,256,1408]{1,0,2:T(8,128)(2,1)} %copy.38, f32[16,1408]{0,1:T(8,128)S(1)} %copy-done.2), kind=kLoop, calls=%fused_computation | loop fusion | flops 23068672 | bytes 46227456 | tf_op jit(solution)/shard_map/convert_element_type | solution.py:16
  218.2 0.0 copy-start.3
  218.2 0.0 copy-start.4
  218.2 234.6 %all-to-all-done = bf16[8,16,256,176]{2,3,1,0:T(8,128)(2,1)} async-done(((bf16[8,16,256,176]{2,3,1,0:T(8,128)(2,1)}), bf16[8,16,256,176]{2,3,1,0:T(8,128)(2,1)}, u32[]{:S(2)}, u32[]{:S(2)}) %all-to-all-start) | async-done | bytes 11534368 | tf_op jit(solution)/shard_map/all_to_all | solution.py:20
  452.8 5.3 all-to-all-start.1
  458.1 0.0 copy-done.3
  458.1 0.0 copy-done.4
  458.1 257.3 %all_gather.6 = bf16[2048,16]{0,1:T(8,128)(2,1)S(1)} all-gather(bf16[256,16]{0,1:T(8,128)(2,1)S(1)} %multiply_convert_fusion), channel_id=1, replica_groups=mesh['ep'=4,'fsdp'=8] {'fsdp'}, dimensions={0}, use_global_device_ids=true | all-gather | bytes 73728 | tf_op jit(solution)/shard_map/all_gather | solution.py:34
  715.4 8.9 %all_gather.7 = bf16[2048,64]{0,1:T(8,128)(2,1)S(1)} all-gather(bf16[2048,16]{0,1:T(8,128)(2,1)S(1)} %all_gather.6), channel_id=1, replica_groups=mesh['ep'=4,'fsdp'=8] {'ep'}, dimensions={1}, use_global_device_ids=true | all-gather | bytes 327680 | tf_op jit(solution)/shard_map/all_gather | solution.py:35
  724.4 0.7 copy.42
  725.0 1.4 constant_dynamic-slice_fusion.1
  726.5 10.0 %copy.44 = bf16[8,16,22,8,256]{4,3,0,2,1:T(8,128)(2,1)} copy(bf16[8,16,22,8,256]{4,3,2,1,0:T(8,128)(2,1)} %bitcast.12) | data formatting | bytes 23068672 | tf_op jit(solution)/shard_map/reshape | solution.py:19
  736.5 0.0 all-to-all-done.1
  736.5 11.4 %copy.41 = bf16[16,8,256,176]{2,1,3,0:T(8,128)(2,1)} copy(bf16[16,8,256,176]{2,0,3,1:T(8,128)(2,1)} %bitcast.11) | data formatting | bytes 23068672 | tf_op jit(solution)/shard_map/all_to_all | solution.py:25
  747.8 18.0 %all_to_all.20 = bf16[16,2048,176]{1,2,0:T(8,128)(2,1)} reshape(bf16[16,8,256,176]{2,1,3,0:T(8,128)(2,1)} %copy.41) | data formatting | bytes 23068672 | tf_op jit(solution)/shard_map/all_to_all | solution.py:25
  765.8 0.7 copy.55
  (2 shorter events, 0.0 us)
Async XLA Ops:
  7.2 167.4 %all-reduce.3.cloned.1.call-start = ((), (), s32[]{:S(2)}) async-start(), calls=%async_computation.2 | async-start | bytes 1622016 | tf_op jit(solution)/shard_map/pmax | solution.py:11
  85.5 20.9 %copy-start = (f32[16,256,1408]{1,2,0:T(8,128)S(1)}, f32[16,256,1408]{1,2,0:T(8,128)}, u32[]{:S(2)}) copy-start(f32[16,256,1408]{1,2,0:T(8,128)} %copy.36) | copy-start | bytes 69206016
  85.5 20.9 %copy-start.1 = (bf16[16,256,1408]{1,2,0:T(8,128)(2,1)S(1)}, bf16[16,256,1408]{1,2,0:T(8,128)(2,1)}, u32[]{:S(2)}) copy-start(bf16[16,256,1408]{1,2,0:T(8,128)(2,1)} %copy.35) | copy-start | bytes 34603012
  196.2 5.4 copy-start.2
  196.2 256.7 %all-to-all-start = ((bf16[8,16,256,176]{2,3,1,0:T(8,128)(2,1)}), bf16[8,16,256,176]{2,3,1,0:T(8,128)(2,1)}, u32[]{:S(2)}, u32[]{:S(2)}) async-start(bf16[8,16,256,176]{2,3,1,0:T(8,128)(2,1)} %fusion), calls=%async_computation | async-start | bytes 23068672 | tf_op jit(solution)/shard_map/all_to_all | solution.py:20
  218.2 239.9 %copy-start.3 = (f32[256,16]{0,1:T(8,128)S(1)}, f32[256,16]{0,1:T(8,128)}, u32[]{:S(2)}) copy-start(f32[256,16]{0,1:T(8,128)} %param.10) | copy-start | bytes 49156
  218.2 239.9 %copy-start.4 = (f32[256]{0:T(256)S(1)}, f32[256]{0:T(256)}, u32[]{:S(2)}) copy-start(f32[256]{0:T(256)} %param.11) | copy-start | bytes 3076
  452.8 283.6 %all-to-all-start.1 = ((bf16[16,256,1408]{1,0,2:T(8,128)(2,1)}), bf16[16,256,1408]{1,0,2:T(8,128)(2,1)}, u32[]{:S(2)}, u32[]{:S(2)}) async-start(bf16[16,256,1408]{1,0,2:T(8,128)(2,1)} %divide_convert_fusion), calls=%async_computation.1 | async-start | bytes 23068672 | tf_op jit(solution)/shard_map/all_to_all | solution.py:25
Sparse Core Ops, SparseCore 0:
  114.4 60.0 all-reduce.2
